TPU v7x, 32 devices: a whole 2x2x4 slice. The times are simulated.
32 devices in a mesh: groups: 2 (over y), center: 8 (over z, x), row: 2 (over core).
Axes of the slice: x: 2, y: 2, z: 4, core: 2. Of those that a mesh axis runs over, the one named last changes fastest.
Arguments:
- dataset: float32 [512, 1024], P(('groups', 'center', 'row')), parts along dimension 0, may hold values from -0.1875 to 0.1875
- centers: float32 [2048, 1024], P(('groups', 'center')), parts along dimension 0, may hold values from -0.1875 to 0.1875
- weights: float32 [2048, 512], P(('groups', 'center'), 'row'), parts along dimension 0, may hold values from -0.1875 to 0.1875
- batch_index: int32 [2, 128], P(None, ('groups', 'center', 'row')), parts along dimension 1, may hold values from 0 to 15
- targets: float32 [2, 128, 512], P(None, ('groups', 'center', 'row')), parts along dimension 1, may hold values from -6 to 6
- gamma: float32 [2], P('groups'), parts along dimension 0, may hold values from 0.3 to 1.5
Outputs:
- new_weights: float32 [2048, 512], P(('groups', 'center'), 'row'), parts along dimension 0
- residual: float32 [128, 512], P(('groups', 'center', 'row')), parts along dimension 0
There are 2 independent parts, one for each index of `groups`. A program takes and returns all parts, laid end to end along the dimension named above; each array names one. Nothing has to cross between parts.
Inputs may be any that keep to these rules, and one draw needn't show every extreme that they name: `batch_index`: each entry picks a row within the block of 16 dataset rows that has the same block number as the entry's block of 4 batch rows.
All inputs are finite; a program needn't handle non-finite values.
Results may differ from a plain program's by a relative error of at most 0.0001.
Values sent between devices are 32-bit elements; how exact they have to be, the bound alone decides.
No kernel may reach another device: no remote copies, remote signals or barrier semaphores. Data moves between devices by JAX's collectives and lax.ppermute only.
A program may use at most 64 MiB of HBM per device.

v0:
```python
import jax
import jax.numpy as jnp
from jax import lax
from jax.sharding import PartitionSpec as P


def per_device(dataset, centers, weights, batch_index, targets, gamma):
    center_sq = jnp.sum(centers * centers, axis=1)
    rows_here = batch_index.shape[1]
    current = weights
    residual = None
    for step in range(2):
        local_rows = dataset[batch_index[step]]
        rows, wanted = (
            lax.all_gather(local_rows, "center", axis=0, tiled=True),
            lax.all_gather(targets[step], "center", axis=0, tiled=True),
        )
        full_weights = lax.all_gather(current, "row", axis=1, tiled=True)
        row_sq = jnp.sum(rows * rows, axis=1)
        cross = jnp.dot(
            rows, centers.T, precision=lax.Precision.HIGHEST, preferred_element_type=jnp.float32
        )
        kernel = jnp.exp(-gamma[0] * (row_sq[:, None] + center_sq[None, :] - 2.0 * cross))
        partial_pred = jnp.dot(
            kernel,
            full_weights,
            precision=lax.Precision.HIGHEST,
            preferred_element_type=jnp.float32,
        )
        summed = lax.psum(partial_pred, "center")
        gathered_res = summed - wanted
        residual = lax.dynamic_slice_in_dim(
            gathered_res, lax.axis_index("center") * rows_here, rows_here, 0
        )
        grad = jnp.dot(
            kernel.T,
            gathered_res,
            precision=lax.Precision.HIGHEST,
            preferred_element_type=jnp.float32,
        )
        own_grad = lax.psum_scatter(grad, "row", scatter_dimension=1, tiled=True)
        batch_total = rows.shape[0] * lax.axis_size("row")
        current = current - 0.5 / batch_total * own_grad
    return (current, residual)


def solution(mesh):
    return jax.shard_map(
        per_device,
        mesh=mesh,
        in_specs=(
            P(("groups", "center", "row"), None),
            P(("groups", "center"), None),
            P(("groups", "center"), "row"),
            P(None, ("groups", "center", "row")),
            P(None, ("groups", "center", "row"), None),
            P("groups"),
        ),
        out_specs=(P(("groups", "center"), "row"), P(("groups", "center", "row"), None)),
        check_vma=False,
    )
```

profile of v0, /device:TPU:0, one launch (start us, length us, event | category | flops | bytes accessed | tf_op | source)
XLA Modules:
  0.0 241.9 jit_solution(545532573906874737)
XLA Ops:
  7.9 1.2 multiply_reduce_fusion
  9.1 0.6 gather_fusion
  9.7 32.3 %all-gather.4 = f32[8,4,1024]{2,1,0:T(4,128)S(1)} all-gather(f32[1,4,1024]{2,1,0:T(4,128)S(1)} %bitcast.27), channel_id=2, replica_groups=mesh['groups'=2,'center'=8,'row'=2] {'center'}, dimensions={0}, use_global_device_ids=true | all-gather | bytes 147456 | tf_op jit(solution)/shard_map/all_gather | solution.py:15
  42.2 0.8 copy-done.2
  43.0 2.0 all_gather.19
  44.9 0.6 fusion.5
  45.6 0.9 fusion.11
  46.5 0.6 copy-done.3
  47.2 30.5 %all-gather.1 = f32[1,32,512]{2,0,1:T(1,128)S(1)} all-gather(f32[1,4,512]{2,0,1:T(1,128)S(1)} %copy.12), channel_id=3, replica_groups=mesh['groups'=2,'center'=8,'row'=2] {'center'}, dimensions={1}, use_global_device_ids=true | all-gather | bytes 73728 | tf_op jit(solution)/shard_map/all_gather | solution.py:16
  77.7 39.1 %all-reduce.3.cloned.1.call-done = f32[32,512]{1,0:T(8,128)} async-done(((f32[32,512]{1,0:T(8,128)}), f32[32,512]{1,0:T(8,128)}) %all-reduce.3.cloned.1.call-update) | async-done | bytes 65552 | tf_op jit(solution)/shard_map/psum | solution.py:30
  116.8 2.0 fusion.6
  118.8 0.6 gather_fusion.1
  119.4 30.5 %all-gather.5 = f32[8,4,1024]{2,1,0:T(4,128)S(1)} all-gather(f32[1,4,1024]{2,1,0:T(4,128)S(1)} %bitcast.28), channel_id=4, replica_groups=mesh['groups'=2,'center'=8,'row'=2] {'center'}, dimensions={0}, use_global_device_ids=true | all-gather | bytes 147456 | tf_op jit(solution)/shard_map/all_gather | solution.py:15
  150.1 0.6 fusion.2
  150.8 0.9 multiply_subtract_fusion.1
  151.7 2.0 all_gather.22
  153.7 0.9 fusion.12
  154.7 30.5 %all-gather.3 = f32[1,32,512]{2,0,1:T(1,128)S(1)} all-gather(f32[1,4,512]{2,0,1:T(1,128)S(1)} %copy.13), channel_id=5, replica_groups=mesh['groups'=2,'center'=8,'row'=2] {'center'}, dimensions={1}, use_global_device_ids=true | all-gather | bytes 73728 | tf_op jit(solution)/shard_map/all_gather | solution.py:16
  185.2 38.8 %all-reduce.5.cloned.1.call-done = f32[32,512]{1,0:T(8,128)} async-done(((f32[32,512]{1,0:T(8,128)}), f32[32,512]{1,0:T(8,128)}) %all-reduce.5.cloned.1.call-update) | async-done | bytes 65552 | tf_op jit(solution)/shard_map/psum | solution.py:30
  224.0 0.8 bitcast_subtract_fusion
  224.8 1.1 fusion.13
  226.0 0.6 constant_dynamic-slice_fusion
  226.6 7.2 %reduce-scatter.5.cloned.1.call-done = f32[128,256]{1,0:T(8,128)} async-done(((f32[128,512]{1,0:T(8,128)}), f32[128,256]{1,0:T(8,128)}) %reduce-scatter.5.cloned.1.call-update) | async-done | bytes 131088 | tf_op jit(solution)/shard_map/reduce_scatter | solution.py:41
  233.8 1.6 multiply_subtract_fusion
  (26 shorter events, 0.6 us)
Async XLA Ops:
  7.2 1.9 copy-start
  7.2 109.6 %all-reduce.3.cloned.1.call-start = ((), (), s32[]{:S(2)}) async-start(), calls=%async_computation.2 | async-start | bytes 131072 | tf_op jit(solution)/shard_map/psum | solution.py:30
  7.9 1.2 copy-start.4
  9.1 35.9 %copy-start.1 = (f32[128,1024]{1,0:T(8,128)S(1)}, f32[128,1024]{1,0:T(8,128)}, u32[]{:S(2)}) copy-start(f32[128,1024]{1,0:T(8,128)} %param.7) | copy-start | bytes 1572868
  42.1 0.9 copy-start.2
  46.5 0.7 copy-start.3
  46.5 104.3 %reduce-scatter.3.cloned.1.call-start = ((), (), s32[]{:S(2)}) async-start(), calls=%async_computation.3 | async-start | bytes 393216 | tf_op jit(solution)/shard_map/reduce_scatter | solution.py:41
  118.8 105.2 %all-reduce.5.cloned.1.call-start = ((), (), s32[]{:S(2)}) async-start(), calls=%async_computation.4 | async-start | bytes 131072 | tf_op jit(solution)/shard_map/psum | solution.py:30
  154.6 79.2 %reduce-scatter.5.cloned.1.call-start = ((), (), s32[]{:S(2)}) async-start(), calls=%async_computation.5 | async-start | bytes 393216 | tf_op jit(solution)/shard_map/reduce_scatter | solution.py:41
Sparse Core Ops, SparseCore 0:
  46.6 70.1 all-reduce.2
  119.0 7.6 reduce-scatter.2
  154.7 69.2 all-reduce.4
  226.1 7.6 reduce-scatter.4
where the time goes:
time: 242 us
  blocking collectives  128 us (53%)
  waiting for transfers between devices  85.2 us (35%)
  between operations  14.5 us (6%)
  matrix products  6.1 us (3%)
  other arithmetic  4.76 us (2%)
  local copies, waits for them, and re-layouts  3.3 us (1%)
    psum x2, waiting for transfers between devices, per_device(): summed = lax.psum(partial_pred, 'center')  77.8 us
    all_gather x2, blocking collectives, per_device(): lax.all_gather(local_rows, 'center', axis=0, tiled=True)  62.9 us
    all_gather x2, blocking collectives, per_device(): lax.all_gather(targets[step], 'center', axis=0, tiled=True)  61.1 us
    reduce_scatter x2, waiting for transfers between devices, per_device(): own_grad = lax.psum_scatter(grad, 'row', scatter_dimension=1, tiled=True)  7.25 us
  transfers between devices with their start and end apart: 4, of which 3 were waited for; matrix products, arithmetic and copies ran while one was open for 1% of the time, Pallas kernels for 0%

commit v1 on v0

--- a/solution.py
+++ b/solution.py
@@ -27,7 +27,7 @@
             precision=lax.Precision.HIGHEST,
             preferred_element_type=jnp.float32,
         )
-        summed = lax.psum(partial_pred, "center")
+        summed = jnp.sum(lax.all_gather(partial_pred, "center"), axis=0)
         gathered_res = summed - wanted
         residual = lax.dynamic_slice_in_dim(
             gathered_res, lax.axis_index("center") * rows_here, rows_here, 0

time: 242 us -> 224 us (0.926)
  waiting for transfers between devices: 85.2 us -> 8.23 us
  blocking collectives: 128 us -> 191 us
    psum x2 -> x0, waiting for transfers between devices: 77.8 us -> none  [per_device(): summed = lax.psum(partial_pred, 'center')]
    all_gather x0 -> x2, blocking collectives: none -> 62.8 us  [per_device(): summed = jnp.sum(lax.all_gather(partial_pred, 'center'), axis=0)]
  transfers between devices with their start and end apart: 4 -> 2, of which waited for: 3 -> 1; matrix products, arithmetic and copies ran while one was open for 1% -> 1% of each run, Pallas kernels for 0% -> 0%
where the time goes in v1:
time: 224 us
  blocking collectives  191 us (85%)
  between operations  14.8 us (7%)
  waiting for transfers between devices  8.23 us (4%)
  matrix products  3.97 us (2%)
  other arithmetic  3.7 us (2%)
  local copies, waits for them, and re-layouts  2.66 us (1%)
    all_gather x2, blocking collectives, per_device(): lax.all_gather(local_rows, 'center', axis=0, tiled=True)  62.9 us
    all_gather x2, blocking collectives, per_device(): summed = jnp.sum(lax.all_gather(partial_pred, 'center'), axis=0)  62.8 us
    all_gather x2, blocking collectives, per_device(): lax.all_gather(targets[step], 'center', axis=0, tiled=True)  61.1 us
    reduce_scatter x2, waiting for transfers between devices, per_device(): own_grad = lax.psum_scatter(grad, 'row', scatter_dimension=1, tiled=True)  8.2 us
  transfers between devices with their start and end apart: 2, of which 1 were waited for; matrix products, arithmetic and copies ran while one was open for 1% of the time, Pallas kernels for 0%

profile of v1, /device:TPU:0, one launch (start us, length us, event | category | flops | bytes accessed | tf_op | source)
XLA Modules:
  0.0 224.2 jit_solution(14686264214478952327)
XLA Ops:
  7.2 0.8 fusion.9
  8.0 0.6 gather_fusion
  8.6 32.3 %all-gather.6 = f32[8,4,1024]{2,1,0:T(4,128)S(1)} all-gather(f32[1,4,1024]{2,1,0:T(4,128)S(1)} %bitcast.31), channel_id=2, replica_groups=mesh['groups'=2,'center'=8,'row'=2] {'center'}, dimensions={0}, use_global_device_ids=true | all-gather | bytes 147456 | tf_op jit(solution)/shard_map/all_gather | solution.py:15
  41.0 0.1 multiply_reduce_fusion.2
  41.8 0.1 multiply_reduce_fusion
  41.9 0.8 copy-done.2
  42.7 2.0 all_gather.31
  44.6 0.6 fusion.5
  45.3 0.2 fusion.11
  45.5 31.4 %all-gather.1 = f32[256,512]{1,0:T(8,128)S(1)} all-gather(f32[32,512]{1,0:T(8,128)S(1)} %fusion.11), channel_id=3, replica_groups=mesh['groups'=2,'center'=8,'row'=2] {'center'}, dimensions={0}, use_global_device_ids=true | all-gather | bytes 589824 | tf_op jit(solution)/shard_map/all_gather | solution.py:30
  77.0 30.5 %all-gather.2 = f32[1,32,512]{2,0,1:T(1,128)S(1)} all-gather(f32[1,4,512]{2,0,1:T(1,128)S(1)} %copy.12), channel_id=4, replica_groups=mesh['groups'=2,'center'=8,'row'=2] {'center'}, dimensions={1}, use_global_device_ids=true | all-gather | bytes 73728 | tf_op jit(solution)/shard_map/all_gather | solution.py:16
  107.6 1.1 fusion.6
  108.7 0.6 gather_fusion.1
  109.3 30.5 %all-gather.7 = f32[8,4,1024]{2,1,0:T(4,128)S(1)} all-gather(f32[1,4,1024]{2,1,0:T(4,128)S(1)} %bitcast.32), channel_id=5, replica_groups=mesh['groups'=2,'center'=8,'row'=2] {'center'}, dimensions={0}, use_global_device_ids=true | all-gather | bytes 147456 | tf_op jit(solution)/shard_map/all_gather | solution.py:15
  139.9 30.5 %all-gather.5 = f32[1,32,512]{2,0,1:T(1,128)S(1)} all-gather(f32[1,4,512]{2,0,1:T(1,128)S(1)} %copy.13), channel_id=7, replica_groups=mesh['groups'=2,'center'=8,'row'=2] {'center'}, dimensions={1}, use_global_device_ids=true | all-gather | bytes 73728 | tf_op jit(solution)/shard_map/all_gather | solution.py:16
  170.6 0.6 fusion.2
  171.2 0.9 multiply_subtract_fusion.1
  172.2 2.0 all_gather.36
  174.1 0.2 fusion.12
  174.4 31.4 %all-gather.4 = f32[256,512]{1,0:T(8,128)S(1)} all-gather(f32[32,512]{1,0:T(8,128)S(1)} %fusion.12), channel_id=6, replica_groups=mesh['groups'=2,'center'=8,'row'=2] {'center'}, dimensions={0}, use_global_device_ids=true | all-gather | bytes 589824 | tf_op jit(solution)/shard_map/all_gather | solution.py:30
  205.8 1.1 fusion.13
  207.0 0.6 constant_dynamic-slice_fusion
  207.6 8.2 %reduce-scatter.5.cloned.1.call-done = f32[128,256]{1,0:T(8,128)} async-done(((f32[128,512]{1,0:T(8,128)}), f32[128,256]{1,0:T(8,128)}) %reduce-scatter.5.cloned.1.call-update) | async-done | bytes 131088 | tf_op jit(solution)/shard_map/reduce_scatter | solution.py:41
  215.8 1.6 multiply_subtract_fusion
  (22 shorter events, 0.5 us)
Async XLA Ops:
  7.2 0.8 copy-start
  7.2 34.6 %copy-start.1 = (f32[128,1024]{1,0:T(8,128)S(1)}, f32[128,1024]{1,0:T(8,128)}, u32[]{:S(2)}) copy-start(f32[128,1024]{1,0:T(8,128)} %param.7) | copy-start | bytes 1572868
  7.2 164.0 %reduce-scatter.3.cloned.1.call-start = ((), (), s32[]{:S(2)}) async-start(), calls=%async_computation.2 | async-start | bytes 393216 | tf_op jit(solution)/shard_map/reduce_scatter | solution.py:41
  41.8 0.9 copy-start.2
  45.5 31.4 %copy-start.3 = (f32[2,4,512]{2,1,0:T(4,128)S(1)}, f32[2,4,512]{2,1,0:T(4,128)}, u32[]{:S(2)}) copy-start(f32[2,4,512]{2,1,0:T(4,128)} %param.10) | copy-start | bytes 49156
  108.7 107.1 %reduce-scatter.5.cloned.1.call-start = ((), (), s32[]{:S(2)}) async-start(), calls=%async_computation.3 | async-start | bytes 393216 | tf_op jit(solution)/shard_map/reduce_scatter | solution.py:41
Sparse Core Ops, SparseCore 0:
  108.8 8.5 reduce-scatter.2
  207.1 8.6 reduce-scatter.4
